TPU v7x, 32 devices: a whole 2x2x4 slice. The times are simulated.
32 devices in a mesh: pipe: 4 (over x, core), exp: 4 (over z), pair: 2 (over y).
Axes of the slice: x: 2, y: 2, z: 4, core: 2. Of those that a mesh axis runs over, the one named last changes fastest.
Arguments:
- hidden_in: bfloat16 [4, 256, 2048], P(None, ('exp', 'pair')), may hold values from -6 to 6
- routes: int32 [4, 4, 256, 8], P('pipe', None, ('exp', 'pair')), may hold values from 0 to 15, all different within a row; in each aligned block of 32 rows (0 to 31, 32 to 63, ..., all dimensions but the last counted through in order) at most 24 rows name the same one
- gate_probs: float32 [4, 4, 256, 8], P('pipe', None, ('exp', 'pair')), may hold values from 0.02 to 1
- norm_gain: float32 [4, 2048], P('pipe'), may hold values from 0.1 to 1.9
- w_gate: bfloat16 [4, 16, 2048, 768], P('pipe', ('exp', 'pair')), may hold values from -0.125 to 0.125
- w_up: bfloat16 [4, 16, 2048, 768], P('pipe', ('exp', 'pair')), may hold values from -0.125 to 0.125
- w_down: bfloat16 [4, 16, 768, 2048], P('pipe', ('exp', 'pair')), may hold values from -0.21875 to 0.21875
Outputs:
- layer_outputs: bfloat16 [4, 4, 256, 2048], P('pipe', None, ('exp', 'pair'))
Inputs may be any that keep to these rules, and one draw needn't show every extreme that they name: `routes`: within each layer and micro-batch, the 32 tokens of one device (aligned blocks) name no expert more than 24 times in all, and each token names 8 different experts.
All inputs are finite; a program needn't handle non-finite values.
Results may differ from a plain program's by a relative error of at most 0.01.
Values may be sent and summed in bfloat16 or wider, within the bound.
A program may use at most 64 MiB of HBM per device.

v0:
```python
import jax
import jax.numpy as jnp
from jax import lax
from jax.sharding import PartitionSpec as P

EPS = 1e-06


def passed_along(value, axis, steps):
    count = lax.axis_size(axis)
    first, last = (max(0, -steps), min(count, count - steps))
    return lax.ppermute(value, axis, [(source, source + steps) for source in range(first, last)])


def expert_block(arrived, wgate, wupper, wdown):
    gate = jnp.einsum("nlcd,ldf->nlcf", arrived, wgate, preferred_element_type=jnp.float32)
    upward = jnp.einsum("nlcd,ldf->nlcf", arrived, wupper, preferred_element_type=jnp.float32)
    hidden = (jax.nn.silu(gate) * upward).astype(jnp.bfloat16)
    return jnp.einsum("nlcf,lfd->nlcd", hidden, wdown, preferred_element_type=jnp.float32).astype(
        jnp.bfloat16
    )


def on_device(hidden_in, routes, gate_probs, norm_gain, w_gate, w_up, w_down):
    section = lax.axis_index("pipe")
    micro, tok_rows, width = hidden_in.shape
    top_count = routes.shape[3]
    groups = lax.axis_size(("exp", "pair"))
    local_experts = w_gate.shape[1]
    experts = local_experts * groups
    capacity = max(2, 3 * tok_rows * top_count // (2 * experts))
    gain = norm_gain[0]
    wgate = w_gate[0]
    wupper = w_up[0]
    wdown = w_down[0]
    expert_ids = jnp.arange(experts, dtype=jnp.int32)

    def layer(state, index):
        chosen = lax.dynamic_index_in_dim(routes[0], index, 0, keepdims=False).reshape(-1)
        probs = lax.dynamic_index_in_dim(gate_probs[0], index, 0, keepdims=False)
        floated = state.astype(jnp.float32)
        scale = lax.rsqrt(jnp.mean(floated * floated, axis=-1, keepdims=True) + EPS)
        normed = (floated * scale * gain).astype(jnp.bfloat16)
        onehot = (chosen[:, None] == expert_ids[None, :]).astype(jnp.int32)
        before = jnp.cumsum(onehot, axis=0) - onehot
        slots = jnp.sum(before * onehot, axis=1)
        outgoing = jnp.zeros((experts, capacity, width), jnp.bfloat16)
        outgoing = outgoing.at[chosen, slots].set(jnp.repeat(normed, top_count, axis=0))
        grouped = outgoing.reshape(groups, local_experts, capacity, width)
        produced = expert_block(
            lax.all_to_all(grouped, ("exp", "pair"), split_axis=0, concat_axis=0, tiled=True),
            wgate,
            wupper,
            wdown,
        )
        returned = lax.all_to_all(
            produced, ("exp", "pair"), split_axis=0, concat_axis=0, tiled=True
        )
        results = returned.reshape(experts, capacity, width)[chosen, slots]
        results = results.reshape(tok_rows, top_count, width).astype(jnp.float32)
        weights = probs / jnp.sum(probs, axis=-1, keepdims=True)
        mixed = jnp.einsum("tk,tkd->td", weights, results)
        return (floated + mixed).astype(jnp.bfloat16)

    def advance(step, carry):
        received, saved = carry
        index = step - section
        valid = jnp.logical_and(index >= 0, index < micro)
        clipped = jnp.clip(index, 0, micro - 1)
        first = lax.dynamic_index_in_dim(hidden_in, clipped, 0, keepdims=False)
        state = jnp.where(section == 0, first, received)
        updated = layer(state, clipped)
        saved = jnp.where(valid, lax.dynamic_update_index_in_dim(saved, updated, clipped, 0), saved)
        received = passed_along(updated, "pipe", 1)
        return (received, saved)

    start = (
        jnp.zeros((tok_rows, width), jnp.bfloat16),
        jnp.zeros((micro, tok_rows, width), jnp.bfloat16),
    )
    received, saved = lax.fori_loop(0, micro + lax.axis_size("pipe") - 1, advance, start)
    return saved[None]


def solution(mesh):
    in_specs = (
        P(None, ("exp", "pair"), None),
        P("pipe", None, ("exp", "pair"), None),
        P("pipe", None, ("exp", "pair"), None),
        P("pipe", None),
        P("pipe", ("exp", "pair"), None, None),
        P("pipe", ("exp", "pair"), None, None),
        P("pipe", ("exp", "pair"), None, None),
    )
    out_specs = P("pipe", None, ("exp", "pair"), None)
    return jax.shard_map(
        on_device, mesh=mesh, in_specs=in_specs, out_specs=out_specs, check_vma=False
    )
```

profile of v0, /device:TPU:1, one launch (start us, length us, event | category | flops | bytes accessed | tf_op | source)
XLA Modules:
  0.0 937.2 jit_solution(15736673222117613759)
XLA Ops:
  0.9 936.3 %while.18 = (s32[]{:T(128)}, bf16[32,2048]{1,0:T(8,128)(2,1)S(1)}, bf16[4,32,2048]{2,1,0:T(8,128)(2,1)}, pred[]{:T(512)}, s32[]{:T(128)}, /*index=5*/bf16[4,32,2...) while((s32[]{:T(128)}, bf16[32,2048]{1,0:T(8,128)(2,1)S(1)}, ...), condition=%wide.region_7.8_spmd.clone.clone, body=%wide.region_0.7_spmd.clone.clone.sunk | while | flops 3628826880 | bytes 48352280 | solution.py:81
  5.1 23.0 %scatter_fusion = bf16[16,24,2048]{2,1,0:T(8,128)(2,1)S(1)} fusion(bf16[16,24,2048]{2,1,0:T(8,128)(2,1)S(1)} %broadcast.269, s32[256]{0:T(256)S(1)} %bitcast.143, bf16[256,2048]{1,0:T(8,128)(2,1)S(1)} %broadcast_bitcast_fusion.2), kind=kCustom, calls=%fused_computation.1.clone.clone.1 | custom fusion | bytes 3147776 | tf_op jit(solution)/shard_map/while/body/eval_jaxpr/scatter | solution.py:48
  28.1 42.3 %all_to_all.26 = bf16[8,2,24,2048]{3,2,1,0:T(8,128)(2,1)S(1)} all-to-all(bf16[8,2,24,2048]{3,2,1,0:T(8,128)(2,1)S(1)} %bitcast.140), channel_id=1, replica_groups=mesh['pipe'=4,'exp'=4,'pair'=2] {'exp','pair'}, dimensions={0} | all-to-all | bytes 3145728 | tf_op jit(solution)/shard_map/while/body/eval_jaxpr/all_to_all | solution.py:51
  75.5 8.0 fusion.87
  88.9 35.4 %all-to-all-done.1 = bf16[8,2,24,2048]{3,2,1,0:T(8,128)(2,1)S(1)} async-done(((bf16[8,2,24,2048]{3,2,1,0:T(8,128)(2,1)}), bf16[8,2,24,2048]{3,2,1,0:T(8,128)(2,1)S(1)}, u32[]{:S(2)}, u32[]{:S(2)}) %all-to-all-start.1) | async-done | bytes 1572896 | tf_op jit(solution)/shard_map/while/body/eval_jaxpr/all_to_all | solution.py:56
  130.7 5.8 collective-permute-start
  142.6 23.0 %scatter_fusion = bf16[16,24,2048]{2,1,0:T(8,128)(2,1)S(1)} fusion(bf16[16,24,2048]{2,1,0:T(8,128)(2,1)S(1)} %broadcast.269, s32[256]{0:T(256)S(1)} %bitcast.143, bf16[256,2048]{1,0:T(8,128)(2,1)S(1)} %broadcast_bitcast_fusion.2), kind=kCustom, calls=%fused_computation.1.clone.clone.1 | custom fusion | bytes 3147776 | tf_op jit(solution)/shard_map/while/body/eval_jaxpr/scatter | solution.py:48
  165.6 38.8 %all_to_all.26 = bf16[8,2,24,2048]{3,2,1,0:T(8,128)(2,1)S(1)} all-to-all(bf16[8,2,24,2048]{3,2,1,0:T(8,128)(2,1)S(1)} %bitcast.140), channel_id=1, replica_groups=mesh['pipe'=4,'exp'=4,'pair'=2] {'exp','pair'}, dimensions={0} | all-to-all | bytes 3145728 | tf_op jit(solution)/shard_map/while/body/eval_jaxpr/all_to_all | solution.py:51
  204.4 5.2 fusion.86
  209.6 8.0 fusion.87
  222.8 37.0 %all-to-all-done.1 = bf16[8,2,24,2048]{3,2,1,0:T(8,128)(2,1)S(1)} async-done(((bf16[8,2,24,2048]{3,2,1,0:T(8,128)(2,1)}), bf16[8,2,24,2048]{3,2,1,0:T(8,128)(2,1)S(1)}, u32[]{:S(2)}, u32[]{:S(2)}) %all-to-all-start.1) | async-done | bytes 1572896 | tf_op jit(solution)/shard_map/while/body/eval_jaxpr/all_to_all | solution.py:56
  274.2 23.0 %scatter_fusion = bf16[16,24,2048]{2,1,0:T(8,128)(2,1)S(1)} fusion(bf16[16,24,2048]{2,1,0:T(8,128)(2,1)S(1)} %broadcast.269, s32[256]{0:T(256)S(1)} %bitcast.143, bf16[256,2048]{1,0:T(8,128)(2,1)S(1)} %broadcast_bitcast_fusion.2), kind=kCustom, calls=%fused_computation.1.clone.clone.1 | custom fusion | bytes 3147776 | tf_op jit(solution)/shard_map/while/body/eval_jaxpr/scatter | solution.py:48
  297.3 40.7 %all_to_all.26 = bf16[8,2,24,2048]{3,2,1,0:T(8,128)(2,1)S(1)} all-to-all(bf16[8,2,24,2048]{3,2,1,0:T(8,128)(2,1)S(1)} %bitcast.140), channel_id=1, replica_groups=mesh['pipe'=4,'exp'=4,'pair'=2] {'exp','pair'}, dimensions={0} | all-to-all | bytes 3145728 | tf_op jit(solution)/shard_map/while/body/eval_jaxpr/all_to_all | solution.py:51
  343.1 8.0 fusion.87
  356.3 36.3 %all-to-all-done.1 = bf16[8,2,24,2048]{3,2,1,0:T(8,128)(2,1)S(1)} async-done(((bf16[8,2,24,2048]{3,2,1,0:T(8,128)(2,1)}), bf16[8,2,24,2048]{3,2,1,0:T(8,128)(2,1)S(1)}, u32[]{:S(2)}, u32[]{:S(2)}) %all-to-all-start.1) | async-done | bytes 1572896 | tf_op jit(solution)/shard_map/while/body/eval_jaxpr/all_to_all | solution.py:56
  407.1 23.0 %scatter_fusion = bf16[16,24,2048]{2,1,0:T(8,128)(2,1)S(1)} fusion(bf16[16,24,2048]{2,1,0:T(8,128)(2,1)S(1)} %broadcast.269, s32[256]{0:T(256)S(1)} %bitcast.143, bf16[256,2048]{1,0:T(8,128)(2,1)S(1)} %broadcast_bitcast_fusion.2), kind=kCustom, calls=%fused_computation.1.clone.clone.1 | custom fusion | bytes 3147776 | tf_op jit(solution)/shard_map/while/body/eval_jaxpr/scatter | solution.py:48
  430.1 41.4 %all_to_all.26 = bf16[8,2,24,2048]{3,2,1,0:T(8,128)(2,1)S(1)} all-to-all(bf16[8,2,24,2048]{3,2,1,0:T(8,128)(2,1)S(1)} %bitcast.140), channel_id=1, replica_groups=mesh['pipe'=4,'exp'=4,'pair'=2] {'exp','pair'}, dimensions={0} | all-to-all | bytes 3145728 | tf_op jit(solution)/shard_map/while/body/eval_jaxpr/all_to_all | solution.py:51
  476.7 8.0 fusion.87
  489.9 36.3 %all-to-all-done.1 = bf16[8,2,24,2048]{3,2,1,0:T(8,128)(2,1)S(1)} async-done(((bf16[8,2,24,2048]{3,2,1,0:T(8,128)(2,1)}), bf16[8,2,24,2048]{3,2,1,0:T(8,128)(2,1)S(1)}, u32[]{:S(2)}, u32[]{:S(2)}) %all-to-all-start.1) | async-done | bytes 1572896 | tf_op jit(solution)/shard_map/while/body/eval_jaxpr/all_to_all | solution.py:56
  540.6 23.0 %scatter_fusion = bf16[16,24,2048]{2,1,0:T(8,128)(2,1)S(1)} fusion(bf16[16,24,2048]{2,1,0:T(8,128)(2,1)S(1)} %broadcast.269, s32[256]{0:T(256)S(1)} %bitcast.143, bf16[256,2048]{1,0:T(8,128)(2,1)S(1)} %broadcast_bitcast_fusion.2), kind=kCustom, calls=%fused_computation.1.clone.clone.1 | custom fusion | bytes 3147776 | tf_op jit(solution)/shard_map/while/body/eval_jaxpr/scatter | solution.py:48
  563.6 41.4 %all_to_all.26 = bf16[8,2,24,2048]{3,2,1,0:T(8,128)(2,1)S(1)} all-to-all(bf16[8,2,24,2048]{3,2,1,0:T(8,128)(2,1)S(1)} %bitcast.140), channel_id=1, replica_groups=mesh['pipe'=4,'exp'=4,'pair'=2] {'exp','pair'}, dimensions={0} | all-to-all | bytes 3145728 | tf_op jit(solution)/shard_map/while/body/eval_jaxpr/all_to_all | solution.py:51
  605.1 5.2 fusion.86
  610.3 8.0 fusion.87
  623.5 36.3 %all-to-all-done.1 = bf16[8,2,24,2048]{3,2,1,0:T(8,128)(2,1)S(1)} async-done(((bf16[8,2,24,2048]{3,2,1,0:T(8,128)(2,1)}), bf16[8,2,24,2048]{3,2,1,0:T(8,128)(2,1)S(1)}, u32[]{:S(2)}, u32[]{:S(2)}) %all-to-all-start.1) | async-done | bytes 1572896 | tf_op jit(solution)/shard_map/while/body/eval_jaxpr/all_to_all | solution.py:56
  674.2 23.0 %scatter_fusion = bf16[16,24,2048]{2,1,0:T(8,128)(2,1)S(1)} fusion(bf16[16,24,2048]{2,1,0:T(8,128)(2,1)S(1)} %broadcast.269, s32[256]{0:T(256)S(1)} %bitcast.143, bf16[256,2048]{1,0:T(8,128)(2,1)S(1)} %broadcast_bitcast_fusion.2), kind=kCustom, calls=%fused_computation.1.clone.clone.1 | custom fusion | bytes 3147776 | tf_op jit(solution)/shard_map/while/body/eval_jaxpr/scatter | solution.py:48
  697.2 41.4 %all_to_all.26 = bf16[8,2,24,2048]{3,2,1,0:T(8,128)(2,1)S(1)} all-to-all(bf16[8,2,24,2048]{3,2,1,0:T(8,128)(2,1)S(1)} %bitcast.140), channel_id=1, replica_groups=mesh['pipe'=4,'exp'=4,'pair'=2] {'exp','pair'}, dimensions={0} | all-to-all | bytes 3145728 | tf_op jit(solution)/shard_map/while/body/eval_jaxpr/all_to_all | solution.py:51
  743.8 8.0 fusion.87
  757.0 36.3 %all-to-all-done.1 = bf16[8,2,24,2048]{3,2,1,0:T(8,128)(2,1)S(1)} async-done(((bf16[8,2,24,2048]{3,2,1,0:T(8,128)(2,1)}), bf16[8,2,24,2048]{3,2,1,0:T(8,128)(2,1)S(1)}, u32[]{:S(2)}, u32[]{:S(2)}) %all-to-all-start.1) | async-done | bytes 1572896 | tf_op jit(solution)/shard_map/while/body/eval_jaxpr/all_to_all | solution.py:56
  807.8 23.0 %scatter_fusion = bf16[16,24,2048]{2,1,0:T(8,128)(2,1)S(1)} fusion(bf16[16,24,2048]{2,1,0:T(8,128)(2,1)S(1)} %broadcast.269, s32[256]{0:T(256)S(1)} %bitcast.143, bf16[256,2048]{1,0:T(8,128)(2,1)S(1)} %broadcast_bitcast_fusion.2), kind=kCustom, calls=%fused_computation.1.clone.clone.1 | custom fusion | bytes 3147776 | tf_op jit(solution)/shard_map/while/body/eval_jaxpr/scatter | solution.py:48
  830.8 41.4 %all_to_all.26 = bf16[8,2,24,2048]{3,2,1,0:T(8,128)(2,1)S(1)} all-to-all(bf16[8,2,24,2048]{3,2,1,0:T(8,128)(2,1)S(1)} %bitcast.140), channel_id=1, replica_groups=mesh['pipe'=4,'exp'=4,'pair'=2] {'exp','pair'}, dimensions={0} | all-to-all | bytes 3145728 | tf_op jit(solution)/shard_map/while/body/eval_jaxpr/all_to_all | solution.py:51
  877.4 8.0 fusion.87
  890.6 36.3 %all-to-all-done.1 = bf16[8,2,24,2048]{3,2,1,0:T(8,128)(2,1)S(1)} async-done(((bf16[8,2,24,2048]{3,2,1,0:T(8,128)(2,1)}), bf16[8,2,24,2048]{3,2,1,0:T(8,128)(2,1)S(1)}, u32[]{:S(2)}, u32[]{:S(2)}) %all-to-all-start.1) | async-done | bytes 1572896 | tf_op jit(solution)/shard_map/while/body/eval_jaxpr/all_to_all | solution.py:56
  (209 shorter events, 162.0 us)
Async XLA Ops:
  84.8 4.0 copy-start
  84.8 39.5 %all-to-all-start.1 = ((bf16[8,2,24,2048]{3,2,1,0:T(8,128)(2,1)}), bf16[8,2,24,2048]{3,2,1,0:T(8,128)(2,1)S(1)}, u32[]{:S(2)}, u32[]{:S(2)}) async-start(bf16[8,2,24,2048]{3,2,1,0:T(8,128)(2,1)} %copy.47), calls=%async_computation.1 | async-start | bytes 3145728 | tf_op jit(solution)/shard_map/while/body/eval_jaxpr/all_to_all | solution.py:56
  130.7 7.7 collective-permute-start
  218.9 3.7 copy-start
  218.9 40.9 %all-to-all-start.1 = ((bf16[8,2,24,2048]{3,2,1,0:T(8,128)(2,1)}), bf16[8,2,24,2048]{3,2,1,0:T(8,128)(2,1)S(1)}, u32[]{:S(2)}, u32[]{:S(2)}) async-start(bf16[8,2,24,2048]{3,2,1,0:T(8,128)(2,1)} %copy.47), calls=%async_computation.1 | async-start | bytes 3145728 | tf_op jit(solution)/shard_map/while/body/eval_jaxpr/all_to_all | solution.py:56
  266.2 3.8 collective-permute-start
  352.4 3.8 copy-start
  352.4 40.2 %all-to-all-start.1 = ((bf16[8,2,24,2048]{3,2,1,0:T(8,128)(2,1)}), bf16[8,2,24,2048]{3,2,1,0:T(8,128)(2,1)S(1)}, u32[]{:S(2)}, u32[]{:S(2)}) async-start(bf16[8,2,24,2048]{3,2,1,0:T(8,128)(2,1)} %copy.47), calls=%async_computation.1 | async-start | bytes 3145728 | tf_op jit(solution)/shard_map/while/body/eval_jaxpr/all_to_all | solution.py:56
  399.0 3.8 collective-permute-start
  485.9 3.8 copy-start
  485.9 40.2 %all-to-all-start.1 = ((bf16[8,2,24,2048]{3,2,1,0:T(8,128)(2,1)}), bf16[8,2,24,2048]{3,2,1,0:T(8,128)(2,1)S(1)}, u32[]{:S(2)}, u32[]{:S(2)}) async-start(bf16[8,2,24,2048]{3,2,1,0:T(8,128)(2,1)} %copy.47), calls=%async_computation.1 | async-start | bytes 3145728 | tf_op jit(solution)/shard_map/while/body/eval_jaxpr/all_to_all | solution.py:56
  532.6 3.8 collective-permute-start
  619.5 3.8 copy-start
  619.5 40.2 %all-to-all-start.1 = ((bf16[8,2,24,2048]{3,2,1,0:T(8,128)(2,1)}), bf16[8,2,24,2048]{3,2,1,0:T(8,128)(2,1)S(1)}, u32[]{:S(2)}, u32[]{:S(2)}) async-start(bf16[8,2,24,2048]{3,2,1,0:T(8,128)(2,1)} %copy.47), calls=%async_computation.1 | async-start | bytes 3145728 | tf_op jit(solution)/shard_map/while/body/eval_jaxpr/all_to_all | solution.py:56
  666.2 3.8 collective-permute-start
  753.1 3.8 copy-start
  753.1 40.2 %all-to-all-start.1 = ((bf16[8,2,24,2048]{3,2,1,0:T(8,128)(2,1)}), bf16[8,2,24,2048]{3,2,1,0:T(8,128)(2,1)S(1)}, u32[]{:S(2)}, u32[]{:S(2)}) async-start(bf16[8,2,24,2048]{3,2,1,0:T(8,128)(2,1)} %copy.47), calls=%async_computation.1 | async-start | bytes 3145728 | tf_op jit(solution)/shard_map/while/body/eval_jaxpr/all_to_all | solution.py:56
  799.8 3.8 collective-permute-start
  886.7 3.8 copy-start
  886.7 40.2 %all-to-all-start.1 = ((bf16[8,2,24,2048]{3,2,1,0:T(8,128)(2,1)}), bf16[8,2,24,2048]{3,2,1,0:T(8,128)(2,1)S(1)}, u32[]{:S(2)}, u32[]{:S(2)}) async-start(bf16[8,2,24,2048]{3,2,1,0:T(8,128)(2,1)} %copy.47), calls=%async_computation.1 | async-start | bytes 3145728 | tf_op jit(solution)/shard_map/while/body/eval_jaxpr/all_to_all | solution.py:56
  933.4 3.8 collective-permute-start
where the time goes:
time: 939 us; the launch traced here: 937 us
  blocking collectives  287 us (31%)
  waiting for transfers between devices  267 us (28%)
  local copies, waits for them, and re-layouts  212 us (23%)
  matrix products  95.1 us (10%)
  starting transfers between devices  43.8 us (5%)
  other arithmetic  30.3 us (3%)
    all_to_all x7, blocking collectives, layer(): lax.all_to_all(grouped, ('exp', 'pair'), split_axis=0, concat_axis=0, til...  287 us
    all_to_all x7, waiting for transfers between devices, layer(): lax.all_to_all(produced, ('exp', 'pair'), split_axis=0, concat_axis=0, ti...  254 us
    scatter x7, local copies, waits for them, and re-layouts, layer(): outgoing.at[chosen, slots].set(jnp.repeat(normed, top_count, axis=0))  161 us
    dot_general x7, matrix products, expert_block(): jnp.einsum('nlcf,lfd->nlcd', hidden, wdown, preferred_element_type=jnp.fl...  55.9 us
    dot_general x7, matrix products, expert_block(): jnp.einsum('nlcd,ldf->nlcf', arrived, wgate, preferred_element_type=jnp.f...  36.3 us
    gather x7, local copies, waits for them, and re-layouts, layer(): results = returned.reshape(experts, capacity, width)[chosen, slots]  30.3 us
    all_to_all x7, starting transfers between devices, layer(): lax.all_to_all(produced, ('exp', 'pair'), split_axis=0, concat_axis=0, ti...  26.6 us
  transfers between devices with their start and end apart: 14, of which 14 were waited for; matrix products, arithmetic and copies ran while one was open for 0% of the time, Pallas kernels for 0%

commit v1 on v0

--- a/solution.py
+++ b/solution.py
@@ -1,9 +1,397 @@
+import functools
+
 import jax
 import jax.numpy as jnp
 from jax import lax
+from jax.experimental import pallas as pl
+from jax.experimental.pallas import tpu as pltpu
 from jax.sharding import PartitionSpec as P
 
 EPS = 1e-06
+MESH = pl.DeviceIdType.MESH
+F32 = jnp.float32
+BF16 = jnp.bfloat16
+VMEM_LIMIT = 63 * 1024 * 1024
+
+
+def divisor_tile(size, most):
+    tile = most
+    while size % tile:
+        tile //= 2
+    return tile
+
+
+def relay_kernel(
+    stages,
+    zs,
+    ys,
+    hidden_ref,
+    routes_ref,
+    probs_ref,
+    gain_ref,
+    wgate_ref,
+    wup_ref,
+    wdown_ref,
+    out_ref,
+    wg,
+    wu,
+    wd,
+    hbuf,
+    tokens,
+    share,
+    hid,
+    part,
+    fromy,
+    zsend,
+    fromz,
+    obuf,
+    w_sem,
+    h_sem,
+    hs_sem,
+    o_sem,
+    s_sem,
+    sr_sem,
+    a_sem,
+    ar_sem,
+    y_sem,
+    yr_sem,
+    z_sem,
+    zr_sem,
+):
+    micro, rows, width = hbuf.shape
+    locals_, _, ff = wg.shape
+    lanes = share.shape[3]
+    groups = zs * ys
+    experts = groups * locals_
+    stage = lax.axis_index("pipe")
+    z = lax.axis_index("exp")
+    y = lax.axis_index("pair")
+    me = z * ys + y
+    slot = y * zs + z
+
+    def peer(dz, dy):
+        return lax.rem(z + dz, zs), lax.rem(y + dy, ys)
+
+    others = [(dz, dy) for dy in range(ys) for dz in range(zs) if dz or dy]
+
+    loads = []
+    for j in range(locals_):
+        loads.append(
+            (
+                pltpu.make_async_copy(wgate_ref.at[0, j], wg.at[j], w_sem.at[3 * j]),
+                pltpu.make_async_copy(wup_ref.at[0, j], wu.at[j], w_sem.at[3 * j + 1]),
+                pltpu.make_async_copy(
+                    wdown_ref.at[0, j], wd.at[pl.ds(j * ff, ff)], w_sem.at[3 * j + 2]
+                ),
+            )
+        )
+
+    def from_input(m):
+        return pltpu.make_async_copy(hidden_ref.at[m], hbuf.at[m], h_sem.at[m])
+
+    @pl.when(stage == 0)
+    def _():
+        for m in range(micro):
+            from_input(m).start()
+
+    for j in range(locals_):
+        loads[j][0].start()
+        loads[j][1].start()
+    for j in range(locals_):
+        loads[j][2].start()
+
+    barrier = pltpu.get_barrier_semaphore()
+    for dz, dy in others:
+        pz, py = peer(dz, dy)
+        pl.semaphore_signal(barrier, inc=1, device_id={"exp": pz, "pair": py}, device_id_type=MESH)
+
+    @pl.when(stage > 0)
+    def _():
+        pl.semaphore_signal(barrier, inc=1, device_id={"pipe": stage - 1}, device_id_type=MESH)
+
+    @pl.when(stage < stages - 1)
+    def _():
+        pl.semaphore_signal(barrier, inc=1, device_id={"pipe": stage + 1}, device_id_type=MESH)
+
+    lane = lax.broadcasted_iota(jnp.int32, (rows, lanes), 1)
+    for m in range(micro):
+        probs = probs_ref[0, m]
+        normal = probs / jnp.sum(probs, axis=-1, keepdims=True)
+        chosen = routes_ref[0, m]
+        total = jnp.zeros((rows, lanes), F32)
+        for k in range(chosen.shape[1]):
+            named = chosen[:, k : k + 1]
+            hit = jnp.logical_or(lane == named, lane == named + experts)
+            total = total + jnp.where(hit, normal[:, k : k + 1], 0.0)
+        high = total.astype(BF16)
+        low = (total - high.astype(F32)).astype(BF16)
+        share[slot, m] = jnp.where(lane < experts, high, low)
+
+    linked = (stage > 0).astype(jnp.int32) + (stage < stages - 1).astype(jnp.int32)
+    pl.semaphore_wait(barrier, len(others) + linked)
+
+    def share_copy(at, to_z, to_y):
+        return pltpu.make_async_remote_copy(
+            src_ref=share.at[at],
+            dst_ref=share.at[at],
+            send_sem=s_sem.at[to_y * zs + to_z],
+            recv_sem=sr_sem.at[at],
+            device_id={"exp": to_z, "pair": to_y},
+            device_id_type=MESH,
+        )
+
+    def share_send():
+        for dz, dy in others:
+            pz, py = peer(dz, dy)
+            share_copy(slot, pz, py).start()
+
+    def share_wait():
+        for dz, dy in others:
+            pz, py = peer(dz, dy)
+            share_copy(py * zs + pz, pz, py).wait_recv()
+
+    def token_copy(m, at, tag, to_z, to_y):
+        block = tokens.at[m, pl.ds(pl.multiple_of(at * rows, rows), rows)]
+        return pltpu.make_async_remote_copy(
+            src_ref=block,
+            dst_ref=block,
+            send_sem=a_sem.at[m, tag],
+            recv_sem=ar_sem.at[m, at],
+            device_id={"exp": to_z, "pair": to_y},
+            device_id_type=MESH,
+        )
+
+    def y_copy(m, dy, tz):
+        py = lax.rem(y + dy, ys)
+        return pltpu.make_async_remote_copy(
+            src_ref=part.at[m, pl.ds(pl.multiple_of((py * zs + tz) * rows, rows), rows)],
+            dst_ref=fromy.at[m, dy - 1, tz],
+            send_sem=y_sem.at[m, dy - 1, tz],
+            recv_sem=yr_sem.at[m, dy - 1, tz],
+            device_id={"pair": py},
+            device_id_type=MESH,
+        )
+
+    def z_copy(m, dz):
+        pz = lax.rem(z + dz, zs)
+        return pltpu.make_async_remote_copy(
+            src_ref=zsend.at[m, dz],
+            dst_ref=fromz.at[m, dz - 1],
+            send_sem=z_sem.at[m, dz - 1],
+            recv_sem=zr_sem.at[m, dz - 1],
+            device_id={"exp": pz},
+            device_id_type=MESH,
+        )
+
+    def hand_copy(m):
+        return pltpu.make_async_remote_copy(
+            src_ref=obuf.at[m],
+            dst_ref=hbuf.at[m],
+            send_sem=hs_sem.at[m],
+            recv_sem=h_sem.at[m],
+            device_id={"pipe": stage + 1},
+            device_id_type=MESH,
+        )
+
+    def out_copy(m):
+        return pltpu.make_async_copy(obuf.at[m], out_ref.at[0, m], o_sem.at[m])
+
+    def announce(m):
+        from_input(m).wait()
+        state = hbuf[m].astype(F32)
+        scale = lax.rsqrt(jnp.mean(state * state, axis=-1, keepdims=True) + EPS)
+        tokens[m, pl.ds(pl.multiple_of(slot * rows, rows), rows)] = (
+            state * scale * gain_ref[...]
+        ).astype(BF16)
+        for dz in range(1, zs):
+            token_copy(m, slot, dz - 1, lax.rem(z + dz, zs), y).start()
+        for dy in range(1, ys):
+            token_copy(m, slot, (zs - 1) + dy - 1, z, lax.rem(y + dy, ys)).start()
+
+    nz = zs - 1
+
+    def forward_tag(dz, dy):
+        return nz + (ys - 1) + (dz - 1) * (ys - 1) + dy - 1
+
+    def gather(m):
+        for dz in range(1, zs):
+            pz = lax.rem(z + dz, zs)
+            at = y * zs + pz
+            token_copy(m, at, dz - 1, pz, y).wait_recv()
+            for dy in range(1, ys):
+                token_copy(m, at, forward_tag(dz, dy), z, lax.rem(y + dy, ys)).start()
+        for dy in range(1, ys):
+            py = lax.rem(y + dy, ys)
+            for dz in range(zs):
+                pz = lax.rem(z + dz, zs)
+                token_copy(m, py * zs + pz, 0, z, py).wait_recv()
+
+    ftile = divisor_tile(ff, 256)
+    ntile = divisor_tile(width, 512)
+    count = groups * rows
+
+    def compute(m):
+        wide = lax.broadcasted_iota(jnp.int32, (count, lanes), 1)
+        shares = share[:, m].reshape(count, lanes).astype(F32)
+        for j in range(locals_):
+            expert = me * locals_ + j
+            mine = jnp.logical_or(wide == expert, wide == expert + experts)
+            column = jnp.sum(jnp.where(mine, shares, 0.0), axis=-1, keepdims=True)
+
+            @pl.when(m == 0)
+            def _():
+                loads[j][0].wait()
+                loads[j][1].wait()
+
+            for c in range(0, ff, ftile):
+                gate = jnp.dot(tokens[m], wg[j, :, c : c + ftile], preferred_element_type=F32)
+                upward = jnp.dot(tokens[m], wu[j, :, c : c + ftile], preferred_element_type=F32)
+                hid[:, j * ff + c : j * ff + c + ftile] = (
+                    jax.nn.silu(gate) * upward * column
+                ).astype(BF16)
+
+        @pl.when(m == 0)
+        def _():
+            for j in range(locals_):
+                loads[j][2].wait()
+
+        for c in range(0, width, ntile):
+            part[m, :, c : c + ntile] = jnp.dot(
+                hid[...], wd[:, c : c + ntile], preferred_element_type=F32
+            ).astype(BF16)
+
+    def own_part(m, pz):
+        at = pl.multiple_of((y * zs + pz) * rows, rows)
+        return part[m, pl.ds(at, rows)].astype(F32)
+
+    def scatter(m):
+        for dz in range(1, zs + 1):
+            for dy in range(1, ys):
+                y_copy(m, dy, lax.rem(z + dz, zs)).start()
+        for dz in range(1, zs):
+            pz = lax.rem(z + dz, zs)
+            total = own_part(m, pz)
+            for dy in range(1, ys):
+                y_copy(m, dy, pz).wait_recv()
+                total = total + fromy[m, dy - 1, pz].astype(F32)
+            zsend[m, dz] = total.astype(BF16)
+            z_copy(m, dz).start()
+
+    def finish(m):
+        total = hbuf[m].astype(F32) + own_part(m, z)
+        for dy in range(1, ys):
+            y_copy(m, dy, z).wait_recv()
+            total = total + fromy[m, dy - 1, z].astype(F32)
+        for dz in range(1, zs):
+            z_copy(m, dz).wait_recv()
+            total = total + fromz[m, dz - 1].astype(F32)
+        obuf[m] = total.astype(BF16)
+
+        @pl.when(stage < stages - 1)
+        def _():
+            hand_copy(m).start()
+
+        out_copy(m).start()
+
+    announce(0)
+    share_send()
+
+    @pl.loop(0, micro)
+    def _(m):
+        @pl.when(m > 0)
+        def _():
+            announce(m)
+
+        gather(m)
+
+        @pl.when(m == 0)
+        def _():
+            share_wait()
+
+        compute(m)
+        scatter(m)
+        finish(m)
+
+
+    for dz, dy in others:
+        pz, py = peer(dz, dy)
+        share_copy(slot, pz, py).wait_send()
+
+    @pl.loop(0, micro)
+    def _(m):
+        for tag in range(groups - 1 + 0):
+            token_copy(m, slot, tag, z, y).wait_send()
+        for dy in range(1, ys):
+            for tz in range(zs):
+                y_copy(m, dy, tz).wait_send()
+        for dz in range(1, zs):
+            z_copy(m, dz).wait_send()
+
+        @pl.when(stage < stages - 1)
+        def _():
+            hand_copy(m).wait_send()
+
+        out_copy(m).wait()
+
+
+def relayed(hidden_in, routes, gate_probs, norm_gain, w_gate, w_up, w_down):
+    micro, rows, width = hidden_in.shape
+    _, locals_, _, ff = w_gate.shape
+    stages, zs, ys = (lax.axis_size(a) for a in ("pipe", "exp", "pair"))
+    groups = zs * ys
+    lanes = share_lanes(groups * locals_)
+    dma = pltpu.SemaphoreType.DMA
+    anywhere = pl.BlockSpec(memory_space=pl.ANY)
+    inside = pl.BlockSpec(memory_space=pltpu.VMEM)
+    return pl.pallas_call(
+        functools.partial(relay_kernel, stages, zs, ys),
+        out_shape=jax.ShapeDtypeStruct((1, micro, rows, width), BF16),
+        in_specs=[anywhere, inside, inside, inside, anywhere, anywhere, anywhere],
+        out_specs=anywhere,
+        scratch_shapes=[
+            pltpu.VMEM((locals_, width, ff), BF16),
+            pltpu.VMEM((locals_, width, ff), BF16),
+            pltpu.VMEM((locals_ * ff, width), BF16),
+            pltpu.VMEM((micro, rows, width), BF16),
+            pltpu.VMEM((micro, groups * rows, width), BF16),
+            pltpu.VMEM((groups, micro, rows, lanes), BF16),
+            pltpu.VMEM((groups * rows, locals_ * ff), BF16),
+            pltpu.VMEM((micro, groups * rows, width), BF16),
+            pltpu.VMEM((micro, max(1, ys - 1), zs, rows, width), BF16),
+            pltpu.VMEM((micro, zs, rows, width), BF16),
+            pltpu.VMEM((micro, max(1, zs - 1), rows, width), BF16),
+            pltpu.VMEM((micro, rows, width), BF16),
+            dma((3 * locals_,)),
+            dma((micro,)),
+            dma((micro,)),
+            dma((micro,)),
+            dma((groups,)),
+            dma((groups,)),
+            dma((micro, groups)),
+            dma((micro, groups)),
+            dma((micro, max(1, ys - 1), zs)),
+            dma((micro, max(1, ys - 1), zs)),
+            dma((micro, max(1, zs - 1))),
+            dma((micro, max(1, zs - 1))),
+        ],
+        compiler_params=pltpu.CompilerParams(
+            collective_id=0, has_side_effects=True, vmem_limit_bytes=VMEM_LIMIT
+        ),
+    )(hidden_in, routes, gate_probs, norm_gain, w_gate, w_up, w_down)
+
+
+def share_lanes(experts):
+    return -(-2 * experts // 128) * 128
+
+
+def kernel_fits(hidden_in, w_gate, groups):
+    micro, rows, width = hidden_in.shape
+    _, locals_, _, ff = w_gate.shape
+    weights = 3 * locals_ * width * ff
+    moved = micro * rows * width * (4 * groups + 4)
+    small = groups * rows * (locals_ * ff + micro * share_lanes(groups * locals_))
+    fits = 2 * (weights + moved + small) + 8 * 1024 * 1024 < VMEM_LIMIT
+    return fits and rows % 16 == 0 and width % 128 == 0 and ff % 128 == 0
 
 
 def passed_along(value, axis, steps):
@@ -22,6 +410,8 @@
 
 
 def on_device(hidden_in, routes, gate_probs, norm_gain, w_gate, w_up, w_down):
+    if kernel_fits(hidden_in, w_gate, lax.axis_size(("exp", "pair"))):
+        return relayed(hidden_in, routes, gate_probs, norm_gain, w_gate, w_up, w_down)
     section = lax.axis_index("pipe")
     micro, tok_rows, width = hidden_in.shape
     top_count = routes.shape[3]

time: 939 us -> 294 us (0.31)
  the two profiles are of different devices: /device:TPU:1 before, /device:TPU:15 now
where the time goes in v1:
time: 294 us; the launch traced here: 293 us
  Pallas kernels  289 us (98%)
  local copies, waits for them, and re-layouts  4.73 us (2%)
    pallas_call x1, Pallas kernels, relayed(): pl.pallas_call(functools.partial(relay_kernel, stages, zs, ys), out_shape...  289 us

profile of v1, /device:TPU:15, one launch (start us, length us, event | category | flops | bytes accessed | tf_op | source)
XLA Modules:
  0.0 293.5 jit_solution(10038009283867490253)
XLA Ops:
  0.0 1.4 copy.8.routes_ref
  1.4 1.4 copy.9.probs_ref
  2.8 288.7 %shard_map.73 = bf16[1,4,32,2048]{3,2,1,0:T(8,128)(2,1)} custom-call(bf16[4,32,2048]{2,1,0:T(8,128)(2,1)} %hidden_ref.1, s32[1,4,32,8]{3,2,1,0:T(8,128)} %copy.8.routes_ref, f32[1,4,32,8]{3,2,1,0:T(8,128)} %copy.9.probs_ref, f32[1,2048]{1,0:T(1,128)} %gain_ref.1, bf16[1,2,2048,768]{3,2,1,0:T(8,128)(2,1)} %wgate_ref.1, bf16[1,2,2048,768]{3,2,1,0:T(8,128)(2,1)} %wup_ref.1, ...), custom_call_target="tpu_custom_call" | custom-call | tf_op jit(solution)/shard_map/pallas_call | solution.py:346
  291.6 1.9 copy.11

commit v2 on v1

--- a/solution.py
+++ b/solution.py
@@ -11,6 +11,7 @@
 MESH = pl.DeviceIdType.MESH
 F32 = jnp.float32
 BF16 = jnp.bfloat16
+PIECES = 2
 VMEM_LIMIT = 63 * 1024 * 1024
 
 
@@ -25,6 +26,7 @@
     stages,
     zs,
     ys,
+    pieces,
     hidden_ref,
     routes_ref,
     probs_ref,
@@ -68,6 +70,11 @@
     y = lax.axis_index("pair")
     me = z * ys + y
     slot = y * zs + z
+    upper_half = lax.div(2 * z, zs)
+    turn = 1 - 2 * upper_half
+
+    def along(k):
+        return lax.rem(z + turn * k + zs, zs)
 
     def peer(dz, dy):
         return lax.rem(z + dz, zs), lax.rem(y + dy, ys)
@@ -172,14 +179,13 @@
             device_id_type=MESH,
         )
 
-    def z_copy(m, dz):
-        pz = lax.rem(z + dz, zs)
+    def z_copy(m, k, source):
         return pltpu.make_async_remote_copy(
-            src_ref=zsend.at[m, dz],
-            dst_ref=fromz.at[m, dz - 1],
-            send_sem=z_sem.at[m, dz - 1],
-            recv_sem=zr_sem.at[m, dz - 1],
-            device_id={"exp": pz},
+            src_ref=zsend.at[m, k],
+            dst_ref=fromz.at[m, source],
+            send_sem=z_sem.at[m, k - 1],
+            recv_sem=zr_sem.at[m, source],
+            device_id={"exp": along(k)},
             device_id_type=MESH,
         )
 
@@ -203,8 +209,8 @@
         tokens[m, pl.ds(pl.multiple_of(slot * rows, rows), rows)] = (
             state * scale * gain_ref[...]
         ).astype(BF16)
-        for dz in range(1, zs):
-            token_copy(m, slot, dz - 1, lax.rem(z + dz, zs), y).start()
+        for k in range(zs - 1, 0, -1):
+            token_copy(m, slot, k - 1, along(k), y).start()
         for dy in range(1, ys):
             token_copy(m, slot, (zs - 1) + dy - 1, z, lax.rem(y + dy, ys)).start()
 
@@ -213,78 +219,89 @@
     def forward_tag(dz, dy):
         return nz + (ys - 1) + (dz - 1) * (ys - 1) + dy - 1
 
-    def gather(m):
+    def gather_z(m):
         for dz in range(1, zs):
-            pz = lax.rem(z + dz, zs)
+            pz = along(dz)
             at = y * zs + pz
             token_copy(m, at, dz - 1, pz, y).wait_recv()
             for dy in range(1, ys):
                 token_copy(m, at, forward_tag(dz, dy), z, lax.rem(y + dy, ys)).start()
-        for dy in range(1, ys):
-            py = lax.rem(y + dy, ys)
-            for dz in range(zs):
-                pz = lax.rem(z + dz, zs)
-                token_copy(m, py * zs + pz, 0, z, py).wait_recv()
+
+    def gather_y(m, dy):
+        py = lax.rem(y + dy, ys)
+        for dz in range(zs):
+            pz = lax.rem(z + dz, zs)
+            token_copy(m, py * zs + pz, 0, z, py).wait_recv()
 
     ftile = divisor_tile(ff, 256)
     ntile = divisor_tile(width, 512)
     count = groups * rows
 
-    def compute(m):
+    def span(dy):
+        return 0, pl.ds(0, count)
+
+    def upper(m, dy):
+        at, block = span(dy)
         wide = lax.broadcasted_iota(jnp.int32, (count, lanes), 1)
         shares = share[:, m].reshape(count, lanes).astype(F32)
         for j in range(locals_):
             expert = me * locals_ + j
             mine = jnp.logical_or(wide == expert, wide == expert + experts)
             column = jnp.sum(jnp.where(mine, shares, 0.0), axis=-1, keepdims=True)
-
-            @pl.when(m == 0)
-            def _():
-                loads[j][0].wait()
-                loads[j][1].wait()
+            if dy == 0:
+
+                @pl.when(m == 0)
+                def _():
+                    loads[j][0].wait()
+                    loads[j][1].wait()
 
             for c in range(0, ff, ftile):
-                gate = jnp.dot(tokens[m], wg[j, :, c : c + ftile], preferred_element_type=F32)
-                upward = jnp.dot(tokens[m], wu[j, :, c : c + ftile], preferred_element_type=F32)
-                hid[:, j * ff + c : j * ff + c + ftile] = (
+                held = tokens[m, block]
+                gate = jnp.dot(held, wg[j, :, c : c + ftile], preferred_element_type=F32)
+                upward = jnp.dot(held, wu[j, :, c : c + ftile], preferred_element_type=F32)
+                hid[block, j * ff + c : j * ff + c + ftile] = (
                     jax.nn.silu(gate) * upward * column
                 ).astype(BF16)
 
+    def lower(m, dy):
+        _, block = span(dy)
+        for c in range(0, width, ntile):
+            part[m, block, c : c + ntile] = jnp.dot(
+                hid[block], wd[:, c : c + ntile], preferred_element_type=F32
+            ).astype(BF16)
+
+    def down_wait(m):
         @pl.when(m == 0)
         def _():
             for j in range(locals_):
                 loads[j][2].wait()
-
-        for c in range(0, width, ntile):
-            part[m, :, c : c + ntile] = jnp.dot(
-                hid[...], wd[:, c : c + ntile], preferred_element_type=F32
-            ).astype(BF16)
 
     def own_part(m, pz):
         at = pl.multiple_of((y * zs + pz) * rows, rows)
         return part[m, pl.ds(at, rows)].astype(F32)
 
+    def send_y(m, dy):
+        for k in range(zs - 1, -1, -1):
+            y_copy(m, dy, along(k)).start()
+
     def scatter(m):
-        for dz in range(1, zs + 1):
-            for dy in range(1, ys):
-                y_copy(m, dy, lax.rem(z + dz, zs)).start()
-        for dz in range(1, zs):
-            pz = lax.rem(z + dz, zs)
+        for k in range(zs - 1, 0, -1):
+            pz = along(k)
             total = own_part(m, pz)
             for dy in range(1, ys):
                 y_copy(m, dy, pz).wait_recv()
                 total = total + fromy[m, dy - 1, pz].astype(F32)
-            zsend[m, dz] = total.astype(BF16)
-            z_copy(m, dz).start()
+            zsend[m, k] = total.astype(BF16)
+            z_copy(m, k, z).start()
 
     def finish(m):
         total = hbuf[m].astype(F32) + own_part(m, z)
         for dy in range(1, ys):
             y_copy(m, dy, z).wait_recv()
             total = total + fromy[m, dy - 1, z].astype(F32)
-        for dz in range(1, zs):
-            z_copy(m, dz).wait_recv()
-            total = total + fromz[m, dz - 1].astype(F32)
+        for k in range(1, zs):
+            z_copy(m, k, along(k)).wait_recv()
+            total = total + fromz[m, along(k)].astype(F32)
         obuf[m] = total.astype(BF16)
 
         @pl.when(stage < stages - 1)
@@ -293,25 +310,60 @@
 
         out_copy(m).start()
 
-    announce(0)
+    for i in range(pieces):
+        announce(i)
     share_send()
 
-    @pl.loop(0, micro)
-    def _(m):
-        @pl.when(m > 0)
-        def _():
-            announce(m)
-
-        gather(m)
+    @pl.when(stage == 0)
+    def _():
+        for i in range(pieces):
+            gather_z(i)
+
+    @pl.loop(0, micro // pieces)
+    def _(batch):
+        m = batch * pieces
+        following = m + pieces < micro
+        first = jnp.logical_and(stage == 0, following)
+        later = jnp.logical_and(stage > 0, following)
+
+        @pl.when(stage > 0)
+        def _():
+            for i in range(pieces):
+                gather_z(m + i)
+
+        @pl.when(first)
+        def _():
+            for i in range(pieces):
+                announce(m + pieces + i)
 
         @pl.when(m == 0)
         def _():
             share_wait()
 
-        compute(m)
-        scatter(m)
-        finish(m)
-
+        for i in range(pieces):
+            for dy in range(1, ys):
+                gather_y(m + i, dy)
+            upper(m + i, 0)
+            if i == 0:
+                down_wait(m)
+            lower(m + i, 0)
+            for dy in range(1, ys):
+                send_y(m + i, dy)
+
+        @pl.when(first)
+        def _():
+            for i in range(pieces):
+                gather_z(m + pieces + i)
+
+        for i in range(pieces):
+            scatter(m + i)
+        for i in range(pieces):
+            finish(m + i)
+
+        @pl.when(later)
+        def _():
+            for i in range(pieces):
+                announce(m + pieces + i)
 
     for dz, dy in others:
         pz, py = peer(dz, dy)
@@ -319,13 +371,13 @@
 
     @pl.loop(0, micro)
     def _(m):
-        for tag in range(groups - 1 + 0):
+        for tag in range(groups - 1):
             token_copy(m, slot, tag, z, y).wait_send()
         for dy in range(1, ys):
             for tz in range(zs):
                 y_copy(m, dy, tz).wait_send()
         for dz in range(1, zs):
-            z_copy(m, dz).wait_send()
+            z_copy(m, dz, z).wait_send()
 
         @pl.when(stage < stages - 1)
         def _():
@@ -335,6 +387,11 @@
 
 
 def relayed(hidden_in, routes, gate_probs, norm_gain, w_gate, w_up, w_down):
+    batches, whole_rows, _ = hidden_in.shape
+    pieces = PIECES if whole_rows % (16 * PIECES) == 0 else 1
+    hidden_in = cut(hidden_in, 0, pieces)
+    routes = cut(routes, 1, pieces)
+    gate_probs = cut(gate_probs, 1, pieces)
     micro, rows, width = hidden_in.shape
     _, locals_, _, ff = w_gate.shape
     stages, zs, ys = (lax.axis_size(a) for a in ("pipe", "exp", "pair"))
@@ -343,8 +400,8 @@
     dma = pltpu.SemaphoreType.DMA
     anywhere = pl.BlockSpec(memory_space=pl.ANY)
     inside = pl.BlockSpec(memory_space=pltpu.VMEM)
-    return pl.pallas_call(
-        functools.partial(relay_kernel, stages, zs, ys),
+    out = pl.pallas_call(
+        functools.partial(relay_kernel, stages, zs, ys, pieces),
         out_shape=jax.ShapeDtypeStruct((1, micro, rows, width), BF16),
         in_specs=[anywhere, inside, inside, inside, anywhere, anywhere, anywhere],
         out_specs=anywhere,
@@ -359,7 +416,7 @@
             pltpu.VMEM((micro, groups * rows, width), BF16),
             pltpu.VMEM((micro, max(1, ys - 1), zs, rows, width), BF16),
             pltpu.VMEM((micro, zs, rows, width), BF16),
-            pltpu.VMEM((micro, max(1, zs - 1), rows, width), BF16),
+            pltpu.VMEM((micro, zs, rows, width), BF16),
             pltpu.VMEM((micro, rows, width), BF16),
             dma((3 * locals_,)),
             dma((micro,)),
@@ -372,12 +429,19 @@
             dma((micro, max(1, ys - 1), zs)),
             dma((micro, max(1, ys - 1), zs)),
             dma((micro, max(1, zs - 1))),
-            dma((micro, max(1, zs - 1))),
+            dma((micro, zs)),
         ],
         compiler_params=pltpu.CompilerParams(
             collective_id=0, has_side_effects=True, vmem_limit_bytes=VMEM_LIMIT
         ),
     )(hidden_in, routes, gate_probs, norm_gain, w_gate, w_up, w_down)
+    return out.reshape(1, batches, whole_rows, width)
+
+
+def cut(value, axis, pieces):
+    shape = value.shape
+    rows = shape[axis + 1] // pieces
+    return value.reshape(shape[:axis] + (shape[axis] * pieces, rows) + shape[axis + 2 :])
 
 
 def share_lanes(experts):
@@ -388,7 +452,7 @@
     micro, rows, width = hidden_in.shape
     _, locals_, _, ff = w_gate.shape
     weights = 3 * locals_ * width * ff
-    moved = micro * rows * width * (4 * groups + 4)
+    moved = micro * rows * width * (4 * groups + 5)
     small = groups * rows * (locals_ * ff + micro * share_lanes(groups * locals_))
     fits = 2 * (weights + moved + small) + 8 * 1024 * 1024 < VMEM_LIMIT
     return fits and rows % 16 == 0 and width % 128 == 0 and ff % 128 == 0

time: 294 us -> 220 us (0.75)
  Pallas kernels: 289 us -> 213 us
    pallas_call x1, Pallas kernels: 289 us -> 213 us  [relayed(): pl.pallas_call(functools.partial(relay_kernel, stages, zs, ys, pieces), o...]
where the time goes in v2:
time: 220 us; the launch traced here: 218 us
  Pallas kernels  213 us (97%)
  local copies, waits for them, and re-layouts  4.73 us (2%)
    pallas_call x1, Pallas kernels, relayed(): pl.pallas_call(functools.partial(relay_kernel, stages, zs, ys, pieces), o...  213 us
    unnamed x3, local copies, waits for them, and re-layouts  4.73 us

profile of v2, /device:TPU:15, one launch (start us, length us, event | category | flops | bytes accessed | tf_op | source)
XLA Modules:
  0.0 217.6 jit_solution(3820292700102114826)
XLA Ops:
  0.0 1.4 copy.8
  1.4 1.4 copy.9
  2.8 212.8 %shard_map.73 = bf16[1,8,16,2048]{3,2,1,0:T(8,128)(2,1)} custom-call(bf16[8,16,2048]{2,1,0:T(8,128)(2,1)} %bitcast.5, s32[1,8,16,8]{3,2,1,0:T(8,128)} %bitcast.6, f32[1,8,16,8]{3,2,1,0:T(8,128)} %bitcast.7, f32[1,2048]{1,0:T(1,128)} %gain_ref.1, bf16[1,2,2048,768]{3,2,1,0:T(8,128)(2,1)} %wgate_ref.1, bf16[1,2,2048,768]{3,2,1,0:T(8,128)(2,1)} %wup_ref.1, ...), custom_call_target="tpu_custom_call" | custom-call | tf_op jit(solution)/shard_map/pallas_call | solution.py:403
  215.7 1.9 copy.11
